TPU v7x, 32 devices: a whole 2x2x4 slice. The times are simulated.
32 devices in a mesh: snap: 2 (over y), row: 8 (over z, x), col: 2 (over core).
Axes of the slice: x: 2, y: 2, z: 4, core: 2. Of those that a mesh axis runs over, the one named last changes fastest.
Arguments:
- density: bfloat16 [8192, 1024], P(('snap', 'row'), 'col'), parts along dimension 0, may hold values from -0.5 to 2
- pattern: int32 [256, 32], P(('snap', 'row'), 'col'), parts along dimension 0, may hold values 0 or 1
- filter_mask: int32 [256, 32], P(('snap', 'row')), parts along dimension 0, may hold values 0 or 1
Outputs:
- purified: bfloat16 [8192, 1024], P(('snap', 'row'), 'col'), parts along dimension 0
- traces: float32 [4], P('snap'), parts along dimension 0
There are 2 independent parts, one for each index of `snap`. A program takes and returns all parts, laid end to end along the dimension named above; each array names one. Nothing has to cross between parts.
All inputs are finite; a program needn't handle non-finite values. No bound on the sum of `pattern` or of `filter_mask` on one device may be relied on, other than what follows from the above.
Results may differ from a plain program's by a relative error of at most 0.006.
Values may be sent and summed in bfloat16 or wider, within the bound.
A program may use at most 64 MiB of HBM per device.

v0:
```python
import jax
import jax.numpy as jnp
from jax import lax
from jax.sharding import PartitionSpec as P

BLK = 32


def extended_2(value, sides, width):
    for axis, dim in sides:
        size, length = (lax.axis_size(axis), value.shape[dim])
        up = [(i, (i + 1) % size) for i in range(size - 1)]
        down = [(j, i) for i, j in up]
        last = lax.slice_in_dim(value, length - width, length, axis=dim)
        leading = lax.slice_in_dim(value, 0, width, axis=dim)
        before = lax.ppermute(last, axis, up)
        after = lax.ppermute(leading, axis, down)
        value = jnp.concatenate([before, value, after], axis=dim)
    return value


def valid_slots(first_row, row_count, first_slot, slot_count, half_band, block_total):
    row_index = first_row + jnp.arange(row_count, dtype=jnp.int32)
    slot_index = first_slot + jnp.arange(slot_count, dtype=jnp.int32)
    column_index = row_index[:, None] + slot_index[None, :] - half_band
    return ((column_index >= 0) & (column_index < block_total)).astype(jnp.int32)


def expand_mask(values, keep_mask):
    block_rows = keep_mask.shape[0]
    slot_count = keep_mask.shape[1]
    blocks = values.reshape(block_rows, BLK, slot_count, BLK)
    blocks = blocks * keep_mask.astype(values.dtype)[:, None, :, None]
    return blocks.reshape(block_rows * BLK, slot_count * BLK)


def shift_slots(segment, moved):
    height = segment.shape[0]
    if moved > 0:
        return jnp.concatenate(
            [
                jnp.zeros((height, moved * BLK), segment.dtype),
                segment[:, : segment.shape[1] - moved * BLK],
            ],
            1,
        )
    if moved < 0:
        return jnp.concatenate(
            [segment[:, -moved * BLK :], jnp.zeros((height, -moved * BLK), segment.dtype)], 1
        )
    return segment


def band_part(left, extended, first_slot, column_slots, slot_count, half_band):
    block_rows = left.shape[0] // BLK
    byte_limit = 4 * 1024 * 1024
    group_rows = 1
    for candidate in (8, 4, 2):
        if (
            block_rows % candidate == 0
            and candidate * slot_count * BLK * column_slots * BLK * 2 <= byte_limit
        ):
            group_rows = candidate
            break

    def one_group(group):
        first = group * group_rows
        stacked = []
        for offset in range(slot_count):
            segment = lax.dynamic_slice_in_dim(
                extended, (first + offset) * BLK, group_rows * BLK, 0
            )
            segment = shift_slots(segment, offset - half_band)
            segment = lax.dynamic_slice_in_dim(segment, first_slot * BLK, column_slots * BLK, 1)
            stacked.append(segment.reshape(group_rows, BLK, column_slots * BLK))
        gathered = jnp.stack(stacked, 1).reshape(group_rows, slot_count * BLK, column_slots * BLK)
        left_rows = lax.dynamic_slice_in_dim(left, first * BLK, group_rows * BLK, 0).reshape(
            group_rows, BLK, slot_count * BLK
        )
        result = jnp.einsum("gak,gkn->gan", left_rows, gathered, preferred_element_type=jnp.float32)
        return result.reshape(group_rows * BLK, column_slots * BLK)

    result = lax.map(one_group, jnp.arange(block_rows // group_rows, dtype=jnp.int32))
    return result.reshape(block_rows * BLK, column_slots * BLK)


def diagonal_sum(values, chosen):
    block_rows = values.shape[0] // BLK
    slot_total = values.shape[1] // BLK
    diagonal = jnp.diagonal(values.reshape(block_rows, BLK, slot_total, BLK), axis1=1, axis2=3)
    return jnp.sum(diagonal.astype(jnp.float32) * chosen[None, :, None])


def slot_products(
    full_rows, extended, own_filter, first_slot, half_slots, slot_count, half_band, collect
):
    square = band_part(full_rows, extended, first_slot, half_slots, slot_count, half_band)
    squared = expand_mask(square, own_filter).astype(jnp.bfloat16)
    squared_rows = collect(squared)
    cube = band_part(squared_rows, extended, first_slot, half_slots, slot_count, half_band)
    purified = (3.0 * squared.astype(jnp.float32) - 2.0 * expand_mask(cube, own_filter)).astype(
        jnp.bfloat16
    )
    return (purified, squared)


def per_device(density, pattern, filter_mask):
    half_slots = density.shape[1] // BLK
    slot_count = 2 * half_slots
    block_rows = density.shape[0] // BLK
    col_id = lax.axis_index("col")
    row_id = lax.axis_index("row")
    block_total = block_rows * lax.axis_size("row")
    first_slot = col_id * half_slots
    own_valid = valid_slots(
        row_id * block_rows, block_rows, first_slot, half_slots, half_slots, block_total
    )
    kept = expand_mask(density, pattern * own_valid)
    chosen = (first_slot + jnp.arange(half_slots, dtype=jnp.int32) == half_slots).astype(
        jnp.float32
    )
    trace_kept = diagonal_sum(kept, chosen)
    total_kept = lax.psum(trace_kept, ("row", "col"))
    own_filter = lax.dynamic_slice_in_dim(filter_mask, first_slot, half_slots, 1) * own_valid
    rim_rows = extended_2(kept, (("row", 0),), half_slots * BLK)
    extended = lax.all_gather(rim_rows, "col", axis=1, tiled=True)
    full_rows = extended[half_slots * BLK : half_slots * BLK + block_rows * BLK]

    def collect_half(squared):
        return lax.all_gather(squared, "col", axis=1, tiled=True)

    purified, squared = slot_products(
        full_rows,
        extended,
        own_filter,
        first_slot,
        half_slots,
        slot_count,
        half_slots,
        collect_half,
    )
    trace_squared = diagonal_sum(squared, chosen)
    total_squared = lax.psum(trace_squared, ("row", "col"))
    order_total = block_total * BLK
    traces = jnp.stack([total_kept, total_squared]) / order_total
    return (purified, traces)


def solution(mesh):
    return jax.shard_map(
        per_device,
        mesh=mesh,
        in_specs=(P(("snap", "row"), "col"), P(("snap", "row"), "col"), P(("snap", "row"), None)),
        out_specs=(P(("snap", "row"), "col"), P("snap")),
        check_vma=False,
    )
```

profile of v0, /device:TPU:0, one launch (start us, length us, event | category | flops | bytes accessed | tf_op | source)
XLA Modules:
  0.0 517.6 jit_solution(5589783563380693730)
XLA Ops:
  8.4 2.1 mul.804
  10.6 4.9 collective-permute-start
  16.8 21.1 %collective-permute-done = bf16[512,512]{1,0:T(8,128)(2,1)S(1)} collective-permute-done((bf16[512,512]{1,0:T(8,128)(2,1)S(1)}, bf16[512,512]{1,0:T(8,128)(2,1)S(1)}, u32[]{:S(2)}, u32[]{:S(2)}) %collective-permute-start) | collective-permute-done | bytes 524320 | tf_op jit(solution)/shard_map/ppermute | solution.py:16
  40.5 4.3 copy.7
  44.8 2.4 mul.808.clone
  47.2 4.7 mul.809
  51.9 1.8 all-gather.3.cloned.1.call-done
  53.7 2.3 slice.442
  57.1 199.7 %while.26 = (s32[]{:T(128)}, f32[4,128,512]{2,1,0:T(8,128)}, s32[4]{0:T(128)S(1)}, bf16[512,1024]{1,0:T(8,128)(2,1)}, bf16[1536,1024]{1,0:T(8,128)(2,1)}, /*inde...) while((s32[]{:T(128)}, f32[4,128,512]{2,1,0:T(8,128)}, ...), condition=%wide.region_1.2_spmd, body=%wide.region_0.1_spmd.sunk | while | flops 134217904 | bytes 56200764 | solution.py:83
  58.6 1.7 constant_dynamic-slice_fusion.65
  60.3 1.7 constant_dynamic-slice_fusion.66
  65.3 1.6 constant_dynamic-update-slice_fusion.129
  68.4 1.7 constant_dynamic-slice_fusion.67
  103.3 3.0 fusion.27
  108.6 1.7 constant_dynamic-slice_fusion.65
  110.3 1.7 constant_dynamic-slice_fusion.66
  115.2 1.6 constant_dynamic-update-slice_fusion.129
  118.3 1.7 constant_dynamic-slice_fusion.67
  153.2 3.0 fusion.27
  158.5 1.7 constant_dynamic-slice_fusion.65
  160.2 1.7 constant_dynamic-slice_fusion.66
  165.1 1.6 constant_dynamic-update-slice_fusion.129
  168.3 1.7 constant_dynamic-slice_fusion.67
  203.1 3.0 fusion.27
  208.4 1.7 constant_dynamic-slice_fusion.65
  210.1 1.7 constant_dynamic-slice_fusion.66
  215.0 1.6 constant_dynamic-update-slice_fusion.129
  218.2 1.7 constant_dynamic-slice_fusion.67
  253.0 3.0 fusion.27
  256.7 2.5 fusion.4
  259.2 4.6 multiply_bitcast_fusion
  263.8 2.8 gather_fusion
  266.7 2.7 reshape_reshape.10
  269.4 7.3 %copy.8 = f32[16,32,16,32]{2,0,3,1:T(8,128)} copy(f32[16,32,16,32]{3,2,1,0:T(8,128)} %reshape_reshape.10) | data formatting | bytes 2097152 | tf_op jit(solution)/shard_map/reshape;reshape | solution.py:32
  276.6 6.8 %fusion = bf16[16,16,32,32]{1,0,3,2:T(8,128)(2,1)} fusion(f32[16,32,16,32]{2,0,3,1:T(8,128)} %copy.8, f32[16,16]{1,0:T(8,128)S(1)} %get-tuple-element.403), kind=kLoop, calls=%fused_computation.163 | loop fusion | flops 524288 | bytes 1573888 | tf_op jit(solution)/shard_map/jit(diagonal)/transpose | solution.py:90
  283.4 2.8 gather_fusion.1
  287.0 34.8 %all-reduce.62 = (f32[1]{0:T(128)}, f32[1]{0:T(128)}) all-reduce(f32[1]{0:T(128)} %bitcast.140, f32[1]{0:T(128)} %bitcast.138), channel_id=1, replica_groups=mesh['snap'=2,'row'=8,'col'=2] {'row','col'}, use_global_device_ids=true, to_apply=%region_7.8 | all-reduce | flops 2 | bytes 16 | tf_op jit(solution)/shard_map/psum | solution.py:143
  321.9 1.8 maximum_multiply_fusion
  324.8 183.3 %while.27 = (s32[]{:T(128)}, f32[4,128,512]{2,1,0:T(8,128)}, s32[4]{0:T(128)S(1)}, bf16[512,1024]{1,0:T(8,128)(2,1)}, bf16[1536,1024]{1,0:T(8,128)(2,1)S(1)}, /*...) while((s32[]{:T(128)}, f32[4,128,512]{2,1,0:T(8,128)}, ...), condition=%wide.region_3.4_spmd, body=%wide.region_2.3_spmd.sunk | while | flops 134217904 | bytes 43617860 | solution.py:83
  329.9 1.6 constant_dynamic-update-slice_fusion.161
  366.9 3.0 fusion.31
  375.7 1.6 constant_dynamic-update-slice_fusion.161
  412.7 3.0 fusion.31
  421.5 1.6 constant_dynamic-update-slice_fusion.161
  458.5 3.0 fusion.31
  467.3 1.6 constant_dynamic-update-slice_fusion.161
  504.3 3.0 fusion.31
  508.0 2.8 fusion.3
  (710 shorter events, 321.0 us)
Async XLA Ops:
  7.2 46.5 %all-gather.3.cloned.1.call-start = ((), (), s32[]{:S(2)}) async-start(), calls=%async_computation | async-start | bytes 4718592 | tf_op jit(solution)/shard_map/all_gather | solution.py:126
  10.6 27.3 %collective-permute-start = (bf16[512,512]{1,0:T(8,128)(2,1)S(1)}, bf16[512,512]{1,0:T(8,128)(2,1)S(1)}, u32[]{:S(2)}, u32[]{:S(2)}) collective-permute-start(bf16[512,512]{1,0:T(8,128)(2,1)S(1)} %mul.805), channel_id=1, source_target_pairs={{0,2},{2,4},{4,6},{6,8},{8,10},{10,12},{12,14},{1,3},{3,5},{5,7},{... | collective-permute-start | bytes 1572872 | tf_op jit(solution)/shard_map/ppermute | solution.py:16
  15.5 22.4 %collective-permute-start.1 = (bf16[512,512]{1,0:T(8,128)(2,1)S(1)}, bf16[512,512]{1,0:T(8,128)(2,1)S(1)}, u32[]{:S(2)}, u32[]{:S(2)}) collective-permute-start(bf16[512,512]{1,0:T(8,128)(2,1)S(1)} %mul.805), channel_id=1, source_target_pairs={{2,0},{4,2},{6,4},{8,6},{10,8},{12,10},{14,12},{3,1},{5,3},{7,5},{... | collective-permute-start | bytes 1572872 | tf_op jit(solution)/shard_map/ppermute | solution.py:17
  39.2 284.5 %all-gather.5.cloned.1.call-start = ((), (), s32[]{:S(2)}) async-start(), calls=%async_computation.1 | async-start | bytes 1572864 | tf_op jit(solution)/shard_map/all_gather | solution.py:130
  57.1 13.0 %copy-start = (bf16[1536,1024]{1,0:T(8,128)(2,1)S(1)}, bf16[1536,1024]{1,0:T(8,128)(2,1)}, u32[]{:S(2)}) copy-start(bf16[1536,1024]{1,0:T(8,128)(2,1)} %get-tuple-element.866) | copy-start | bytes 9437188 | tf_op jit(solution)/shard_map/while
  87.8 10.0 %copy-start.6 = (bf16[128,704]{1,0:T(8,128)(2,1)S(1)}, bf16[128,704]{1,0:T(8,128)(2,1)}, u32[]{:S(2)}) copy-start(bf16[128,704]{1,0:T(8,128)(2,1)} %get-tuple-element.660) | copy-start | bytes 540676 | tf_op jit(solution)/shard_map/while
  87.8 11.5 %copy-start.18 = (bf16[128,640]{1,0:T(8,128)(2,1)S(1)}, bf16[128,640]{1,0:T(8,128)(2,1)}, u32[]{:S(2)}) copy-start(bf16[128,640]{1,0:T(8,128)(2,1)} %get-tuple-element.664) | copy-start | bytes 491524 | tf_op jit(solution)/shard_map/while
  87.8 11.5 %copy-start.20 = (bf16[128,608]{1,0:T(8,128)(2,1)S(1)}, bf16[128,608]{1,0:T(8,128)(2,1)}, u32[]{:S(2)}) copy-start(bf16[128,608]{1,0:T(8,128)(2,1)} %get-tuple-element.663) | copy-start | bytes 466948 | tf_op jit(solution)/shard_map/while
  88.1 12.7 %copy-start.14 = (bf16[128,576]{1,0:T(8,128)(2,1)S(1)}, bf16[128,576]{1,0:T(8,128)(2,1)}, u32[]{:S(2)}) copy-start(bf16[128,576]{1,0:T(8,128)(2,1)} %get-tuple-element.668) | copy-start | bytes 442372 | tf_op jit(solution)/shard_map/while
  88.1 12.6 %copy-start.16 = (bf16[128,544]{1,0:T(8,128)(2,1)S(1)}, bf16[128,544]{1,0:T(8,128)(2,1)}, u32[]{:S(2)}) copy-start(bf16[128,544]{1,0:T(8,128)(2,1)} %get-tuple-element.667) | copy-start | bytes 417796 | tf_op jit(solution)/shard_map/while
  107.0 13.0 %copy-start = (bf16[1536,1024]{1,0:T(8,128)(2,1)S(1)}, bf16[1536,1024]{1,0:T(8,128)(2,1)}, u32[]{:S(2)}) copy-start(bf16[1536,1024]{1,0:T(8,128)(2,1)} %get-tuple-element.866) | copy-start | bytes 9437188 | tf_op jit(solution)/shard_map/while
  137.7 10.0 %copy-start.6 = (bf16[128,704]{1,0:T(8,128)(2,1)S(1)}, bf16[128,704]{1,0:T(8,128)(2,1)}, u32[]{:S(2)}) copy-start(bf16[128,704]{1,0:T(8,128)(2,1)} %get-tuple-element.660) | copy-start | bytes 540676 | tf_op jit(solution)/shard_map/while
  137.7 11.5 %copy-start.18 = (bf16[128,640]{1,0:T(8,128)(2,1)S(1)}, bf16[128,640]{1,0:T(8,128)(2,1)}, u32[]{:S(2)}) copy-start(bf16[128,640]{1,0:T(8,128)(2,1)} %get-tuple-element.664) | copy-start | bytes 491524 | tf_op jit(solution)/shard_map/while
  137.8 11.5 %copy-start.20 = (bf16[128,608]{1,0:T(8,128)(2,1)S(1)}, bf16[128,608]{1,0:T(8,128)(2,1)}, u32[]{:S(2)}) copy-start(bf16[128,608]{1,0:T(8,128)(2,1)} %get-tuple-element.663) | copy-start | bytes 466948 | tf_op jit(solution)/shard_map/while
  138.1 12.7 %copy-start.14 = (bf16[128,576]{1,0:T(8,128)(2,1)S(1)}, bf16[128,576]{1,0:T(8,128)(2,1)}, u32[]{:S(2)}) copy-start(bf16[128,576]{1,0:T(8,128)(2,1)} %get-tuple-element.668) | copy-start | bytes 442372 | tf_op jit(solution)/shard_map/while
  138.1 12.6 %copy-start.16 = (bf16[128,544]{1,0:T(8,128)(2,1)S(1)}, bf16[128,544]{1,0:T(8,128)(2,1)}, u32[]{:S(2)}) copy-start(bf16[128,544]{1,0:T(8,128)(2,1)} %get-tuple-element.667) | copy-start | bytes 417796 | tf_op jit(solution)/shard_map/while
  156.9 13.0 %copy-start = (bf16[1536,1024]{1,0:T(8,128)(2,1)S(1)}, bf16[1536,1024]{1,0:T(8,128)(2,1)}, u32[]{:S(2)}) copy-start(bf16[1536,1024]{1,0:T(8,128)(2,1)} %get-tuple-element.866) | copy-start | bytes 9437188 | tf_op jit(solution)/shard_map/while
  187.6 10.0 %copy-start.6 = (bf16[128,704]{1,0:T(8,128)(2,1)S(1)}, bf16[128,704]{1,0:T(8,128)(2,1)}, u32[]{:S(2)}) copy-start(bf16[128,704]{1,0:T(8,128)(2,1)} %get-tuple-element.660) | copy-start | bytes 540676 | tf_op jit(solution)/shard_map/while
  187.7 11.5 %copy-start.18 = (bf16[128,640]{1,0:T(8,128)(2,1)S(1)}, bf16[128,640]{1,0:T(8,128)(2,1)}, u32[]{:S(2)}) copy-start(bf16[128,640]{1,0:T(8,128)(2,1)} %get-tuple-element.664) | copy-start | bytes 491524 | tf_op jit(solution)/shard_map/while
  187.7 11.5 %copy-start.20 = (bf16[128,608]{1,0:T(8,128)(2,1)S(1)}, bf16[128,608]{1,0:T(8,128)(2,1)}, u32[]{:S(2)}) copy-start(bf16[128,608]{1,0:T(8,128)(2,1)} %get-tuple-element.663) | copy-start | bytes 466948 | tf_op jit(solution)/shard_map/while
  188.0 12.7 %copy-start.14 = (bf16[128,576]{1,0:T(8,128)(2,1)S(1)}, bf16[128,576]{1,0:T(8,128)(2,1)}, u32[]{:S(2)}) copy-start(bf16[128,576]{1,0:T(8,128)(2,1)} %get-tuple-element.668) | copy-start | bytes 442372 | tf_op jit(solution)/shard_map/while
  188.0 12.6 %copy-start.16 = (bf16[128,544]{1,0:T(8,128)(2,1)S(1)}, bf16[128,544]{1,0:T(8,128)(2,1)}, u32[]{:S(2)}) copy-start(bf16[128,544]{1,0:T(8,128)(2,1)} %get-tuple-element.667) | copy-start | bytes 417796 | tf_op jit(solution)/shard_map/while
  206.8 13.0 %copy-start = (bf16[1536,1024]{1,0:T(8,128)(2,1)S(1)}, bf16[1536,1024]{1,0:T(8,128)(2,1)}, u32[]{:S(2)}) copy-start(bf16[1536,1024]{1,0:T(8,128)(2,1)} %get-tuple-element.866) | copy-start | bytes 9437188 | tf_op jit(solution)/shard_map/while
  237.5 10.0 %copy-start.6 = (bf16[128,704]{1,0:T(8,128)(2,1)S(1)}, bf16[128,704]{1,0:T(8,128)(2,1)}, u32[]{:S(2)}) copy-start(bf16[128,704]{1,0:T(8,128)(2,1)} %get-tuple-element.660) | copy-start | bytes 540676 | tf_op jit(solution)/shard_map/while
  237.6 11.5 %copy-start.18 = (bf16[128,640]{1,0:T(8,128)(2,1)S(1)}, bf16[128,640]{1,0:T(8,128)(2,1)}, u32[]{:S(2)}) copy-start(bf16[128,640]{1,0:T(8,128)(2,1)} %get-tuple-element.664) | copy-start | bytes 491524 | tf_op jit(solution)/shard_map/while
  237.6 11.5 %copy-start.20 = (bf16[128,608]{1,0:T(8,128)(2,1)S(1)}, bf16[128,608]{1,0:T(8,128)(2,1)}, u32[]{:S(2)}) copy-start(bf16[128,608]{1,0:T(8,128)(2,1)} %get-tuple-element.663) | copy-start | bytes 466948 | tf_op jit(solution)/shard_map/while
  237.9 12.7 %copy-start.14 = (bf16[128,576]{1,0:T(8,128)(2,1)S(1)}, bf16[128,576]{1,0:T(8,128)(2,1)}, u32[]{:S(2)}) copy-start(bf16[128,576]{1,0:T(8,128)(2,1)} %get-tuple-element.668) | copy-start | bytes 442372 | tf_op jit(solution)/shard_map/while
  237.9 12.6 %copy-start.16 = (bf16[128,544]{1,0:T(8,128)(2,1)S(1)}, bf16[128,544]{1,0:T(8,128)(2,1)}, u32[]{:S(2)}) copy-start(bf16[128,544]{1,0:T(8,128)(2,1)} %get-tuple-element.667) | copy-start | bytes 417796 | tf_op jit(solution)/shard_map/while
  276.6 48.1 %copy-start.1 = (bf16[1536,1024]{1,0:T(8,128)(2,1)S(1)}, bf16[1536,1024]{1,0:T(8,128)(2,1)}, u32[]{:S(2)}) copy-start(bf16[1536,1024]{1,0:T(8,128)(2,1)} %get-tuple-element.1109) | copy-start | bytes 9437188
  351.4 10.0 %copy-start.7 = (bf16[128,704]{1,0:T(8,128)(2,1)S(1)}, bf16[128,704]{1,0:T(8,128)(2,1)}, u32[]{:S(2)}) copy-start(bf16[128,704]{1,0:T(8,128)(2,1)} %get-tuple-element.729) | copy-start | bytes 540676 | tf_op jit(solution)/shard_map/while
  351.4 11.5 %copy-start.19 = (bf16[128,640]{1,0:T(8,128)(2,1)S(1)}, bf16[128,640]{1,0:T(8,128)(2,1)}, u32[]{:S(2)}) copy-start(bf16[128,640]{1,0:T(8,128)(2,1)} %get-tuple-element.733) | copy-start | bytes 491524 | tf_op jit(solution)/shard_map/while
  351.4 11.5 %copy-start.21 = (bf16[128,608]{1,0:T(8,128)(2,1)S(1)}, bf16[128,608]{1,0:T(8,128)(2,1)}, u32[]{:S(2)}) copy-start(bf16[128,608]{1,0:T(8,128)(2,1)} %get-tuple-element.732) | copy-start | bytes 466948 | tf_op jit(solution)/shard_map/while
  351.7 12.6 %copy-start.15 = (bf16[128,576]{1,0:T(8,128)(2,1)S(1)}, bf16[128,576]{1,0:T(8,128)(2,1)}, u32[]{:S(2)}) copy-start(bf16[128,576]{1,0:T(8,128)(2,1)} %get-tuple-element.737) | copy-start | bytes 442372 | tf_op jit(solution)/shard_map/while
  351.7 12.6 %copy-start.17 = (bf16[128,544]{1,0:T(8,128)(2,1)S(1)}, bf16[128,544]{1,0:T(8,128)(2,1)}, u32[]{:S(2)}) copy-start(bf16[128,544]{1,0:T(8,128)(2,1)} %get-tuple-element.736) | copy-start | bytes 417796 | tf_op jit(solution)/shard_map/while
  397.2 10.0 %copy-start.7 = (bf16[128,704]{1,0:T(8,128)(2,1)S(1)}, bf16[128,704]{1,0:T(8,128)(2,1)}, u32[]{:S(2)}) copy-start(bf16[128,704]{1,0:T(8,128)(2,1)} %get-tuple-element.729) | copy-start | bytes 540676 | tf_op jit(solution)/shard_map/while
  397.2 11.5 %copy-start.19 = (bf16[128,640]{1,0:T(8,128)(2,1)S(1)}, bf16[128,640]{1,0:T(8,128)(2,1)}, u32[]{:S(2)}) copy-start(bf16[128,640]{1,0:T(8,128)(2,1)} %get-tuple-element.733) | copy-start | bytes 491524 | tf_op jit(solution)/shard_map/while
  397.2 11.5 %copy-start.21 = (bf16[128,608]{1,0:T(8,128)(2,1)S(1)}, bf16[128,608]{1,0:T(8,128)(2,1)}, u32[]{:S(2)}) copy-start(bf16[128,608]{1,0:T(8,128)(2,1)} %get-tuple-element.732) | copy-start | bytes 466948 | tf_op jit(solution)/shard_map/while
  397.6 12.6 %copy-start.15 = (bf16[128,576]{1,0:T(8,128)(2,1)S(1)}, bf16[128,576]{1,0:T(8,128)(2,1)}, u32[]{:S(2)}) copy-start(bf16[128,576]{1,0:T(8,128)(2,1)} %get-tuple-element.737) | copy-start | bytes 442372 | tf_op jit(solution)/shard_map/while
  397.6 12.6 %copy-start.17 = (bf16[128,544]{1,0:T(8,128)(2,1)S(1)}, bf16[128,544]{1,0:T(8,128)(2,1)}, u32[]{:S(2)}) copy-start(bf16[128,544]{1,0:T(8,128)(2,1)} %get-tuple-element.736) | copy-start | bytes 417796 | tf_op jit(solution)/shard_map/while
  443.1 11.5 %copy-start.19 = (bf16[128,640]{1,0:T(8,128)(2,1)S(1)}, bf16[128,640]{1,0:T(8,128)(2,1)}, u32[]{:S(2)}) copy-start(bf16[128,640]{1,0:T(8,128)(2,1)} %get-tuple-element.733) | copy-start | bytes 491524 | tf_op jit(solution)/shard_map/while
  443.1 11.5 %copy-start.21 = (bf16[128,608]{1,0:T(8,128)(2,1)S(1)}, bf16[128,608]{1,0:T(8,128)(2,1)}, u32[]{:S(2)}) copy-start(bf16[128,608]{1,0:T(8,128)(2,1)} %get-tuple-element.732) | copy-start | bytes 466948 | tf_op jit(solution)/shard_map/while
  443.4 12.6 %copy-start.15 = (bf16[128,576]{1,0:T(8,128)(2,1)S(1)}, bf16[128,576]{1,0:T(8,128)(2,1)}, u32[]{:S(2)}) copy-start(bf16[128,576]{1,0:T(8,128)(2,1)} %get-tuple-element.737) | copy-start | bytes 442372 | tf_op jit(solution)/shard_map/while
  443.4 12.6 %copy-start.17 = (bf16[128,544]{1,0:T(8,128)(2,1)S(1)}, bf16[128,544]{1,0:T(8,128)(2,1)}, u32[]{:S(2)}) copy-start(bf16[128,544]{1,0:T(8,128)(2,1)} %get-tuple-element.736) | copy-start | bytes 417796 | tf_op jit(solution)/shard_map/while
  488.8 10.0 %copy-start.7 = (bf16[128,704]{1,0:T(8,128)(2,1)S(1)}, bf16[128,704]{1,0:T(8,128)(2,1)}, u32[]{:S(2)}) copy-start(bf16[128,704]{1,0:T(8,128)(2,1)} %get-tuple-element.729) | copy-start | bytes 540676 | tf_op jit(solution)/shard_map/while
  488.9 11.5 %copy-start.19 = (bf16[128,640]{1,0:T(8,128)(2,1)S(1)}, bf16[128,640]{1,0:T(8,128)(2,1)}, u32[]{:S(2)}) copy-start(bf16[128,640]{1,0:T(8,128)(2,1)} %get-tuple-element.733) | copy-start | bytes 491524 | tf_op jit(solution)/shard_map/while
  488.9 11.5 %copy-start.21 = (bf16[128,608]{1,0:T(8,128)(2,1)S(1)}, bf16[128,608]{1,0:T(8,128)(2,1)}, u32[]{:S(2)}) copy-start(bf16[128,608]{1,0:T(8,128)(2,1)} %get-tuple-element.732) | copy-start | bytes 466948 | tf_op jit(solution)/shard_map/while
  489.2 12.6 %copy-start.15 = (bf16[128,576]{1,0:T(8,128)(2,1)S(1)}, bf16[128,576]{1,0:T(8,128)(2,1)}, u32[]{:S(2)}) copy-start(bf16[128,576]{1,0:T(8,128)(2,1)} %get-tuple-element.737) | copy-start | bytes 442372 | tf_op jit(solution)/shard_map/while
  489.2 12.6 %copy-start.17 = (bf16[128,544]{1,0:T(8,128)(2,1)S(1)}, bf16[128,544]{1,0:T(8,128)(2,1)}, u32[]{:S(2)}) copy-start(bf16[128,544]{1,0:T(8,128)(2,1)} %get-tuple-element.736) | copy-start | bytes 417796 | tf_op jit(solution)/shard_map/while
  (43 other events, 352.4 us)
Sparse Core Ops, SparseCore 0:
  39.3 14.3 all-gather.2
  259.4 10.2 all-gather.4
where the time goes:
time: 520 us; the launch traced here: 518 us
  local copies, waits for them, and re-layouts  381 us (73%)
  blocking collectives  34.8 us (7%)
  matrix products  23.9 us (5%)
  waiting for transfers between devices  22.9 us (4%)
  other arithmetic  21.4 us (4%)
  between operations  14.2 us (3%)
  loops' own time  13.2 us (3%)
  starting transfers between devices  6.27 us (1%)
    while x416, local copies, waits for them, and re-layouts  178 us
    slice x120, local copies, waits for them, and re-layouts, shift_slots(): segment[:, :segment.shape[1] - moved * BLK]  98.7 us
    dynamic_slice x136, local copies, waits for them, and re-layouts, one_group(): lax.dynamic_slice_in_dim(segment, first_slot * BLK, column_slots * BLK, 1)  45.4 us
    psum x1, blocking collectives, per_device(): total_squared = lax.psum(trace_squared, ('row', 'col'))  34.8 us
    dot_general x8, matrix products, one_group(): jnp.einsum('gak,gkn->gan', left_rows, gathered, preferred_element_type=jn...  23.9 us
    ppermute x1, waiting for transfers between devices, extended_2(): before = lax.ppermute(last, axis, up)  21.1 us
    another operation x2, loops' own time, band_part(): lax.map(one_group, jnp.arange(block_rows // group_rows, dtype=jnp.int32))  13.2 us
    transpose x2, other arithmetic, diagonal_sum(): jnp.diagonal(values.reshape(block_rows, BLK, slot_total, BLK), axis1=1, a...  11.4 us
  transfers between devices with their start and end apart: 4, of which 2 were waited for; matrix products, arithmetic and copies ran while one was open for 8% of the time, Pallas kernels for 0%

commit v1 on v0

v1 whole, which is shorter than its diff:
```python
import functools

import jax
import jax.numpy as jnp
from jax import lax
from jax.experimental import pallas as pl
from jax.experimental.pallas import tpu as pltpu
from jax.sharding import PartitionSpec as P

BLK = 32
LANE = 128
CHUNKS = 8
MESH = pl.DeviceIdType.MESH


def expander(width):
    row = lax.broadcasted_iota(jnp.int32, (LANE, width), 0)
    col = lax.broadcasted_iota(jnp.int32, (LANE, width), 1)
    return (col // BLK == row).astype(jnp.bfloat16)


def lanes_padded(value):
    short = LANE - value.shape[1]
    return jnp.concatenate([value, jnp.zeros((value.shape[0], short), value.dtype)], 1)


def valid_slots(first_row, rows, first_slot, half, total):
    row = lax.broadcasted_iota(jnp.int32, (rows, LANE), 0) + first_row
    slot = lax.broadcasted_iota(jnp.int32, (rows, LANE), 1) + first_slot
    column = row + slot - half
    return ((column >= 0) & (column < total)).astype(jnp.float32)


def kernel(
    row_size,
    density,
    pattern,
    filter_mask,
    out,
    traces,
    kept,
    near,
    right,
    squared,
    keep_filter,
    result,
    part,
    parts,
    send_sem,
    sib_sem,
    p_sem,
    psib_sem,
    q_sem,
    qsib_sem,
    tsend_sem,
    trecv_sem,
):
    rows, width = density.shape
    half = width // BLK
    block_rows = rows // BLK
    chunk = rows // CHUNKS
    snap = lax.axis_index("snap")
    me = lax.axis_index("row")
    core = lax.axis_index("col")
    odd = lax.rem(me, 2)
    partner = me + 1 - 2 * odd
    onward = me + 2 - 4 * odd
    origin = me - 2 + 4 * odd
    has_onward = (onward >= 0) & (onward < row_size)
    has_origin = (origin >= 0) & (origin < row_size)
    p_side = 1 - odd
    q_side = odd
    other = 1 - core
    total = row_size * block_rows

    barrier = pltpu.get_barrier_semaphore()

    def greet(step, _):
        peer = lax.rem(me + step, row_size)
        pl.semaphore_signal(barrier, inc=1, device_id=(snap, peer, core), device_id_type=MESH)
        return 0

    pl.semaphore_signal(barrier, inc=1, device_id=(snap, me, other), device_id_type=MESH)
    lax.fori_loop(1, row_size, greet, 0)

    first_slot = core * half
    keep = lanes_padded(pattern[...]).astype(jnp.float32)
    keep = keep * valid_slots(me * block_rows, block_rows, first_slot, half, total)
    spread = jnp.dot(keep.astype(jnp.bfloat16), expander(width), preferred_element_type=jnp.float32)
    for m in range(block_rows):
        at = pl.ds(m * BLK, BLK)
        kept[core, at, :] = (
            density[at, :].astype(jnp.float32) * spread[m : m + 1, :]
        ).astype(jnp.bfloat16)
    keep = lanes_padded(filter_mask[...]).astype(jnp.float32)
    keep = keep * valid_slots(me * block_rows, block_rows, 0, half, total)
    keep = pltpu.roll(keep, 0, 1, stride=1, stride_axis=0)
    keep_filter[...] = jnp.dot(
        keep.astype(jnp.bfloat16), expander(3 * width), preferred_element_type=jnp.float32
    )
    right[...] = jnp.zeros_like(right)

    pl.semaphore_wait(barrier, row_size)

    def block(k):
        return pl.ds(k * chunk, chunk)

    def to_partner(k):
        return pltpu.make_async_remote_copy(
            src_ref=kept.at[core, block(k), :],
            dst_ref=near.at[odd, core, block(k), :],
            send_sem=send_sem.at[0, k],
            recv_sem=p_sem.at[k],
            device_id=(snap, partner, core),
            device_id_type=MESH,
        )

    def from_partner(k):
        return pltpu.make_async_remote_copy(
            src_ref=kept.at[core, block(k), :],
            dst_ref=near.at[p_side, core, block(k), :],
            send_sem=send_sem.at[0, k],
            recv_sem=p_sem.at[k],
            device_id=(snap, partner, core),
            device_id_type=MESH,
        )

    def to_onward(k):
        return pltpu.make_async_remote_copy(
            src_ref=near.at[p_side, core, block(k), :],
            dst_ref=near.at[q_side, core, block(k), :],
            send_sem=send_sem.at[1, k],
            recv_sem=q_sem.at[k],
            device_id=(snap, onward, core),
            device_id_type=MESH,
        )

    def from_origin(k):
        return pltpu.make_async_remote_copy(
            src_ref=near.at[p_side, core, block(k), :],
            dst_ref=near.at[q_side, core, block(k), :],
            send_sem=send_sem.at[1, k],
            recv_sem=q_sem.at[k],
            device_id=(snap, origin, core),
            device_id_type=MESH,
        )

    def across(side, half_at, k, sent, received):
        return pltpu.make_async_remote_copy(
            src_ref=near.at[side, half_at, block(k), :],
            dst_ref=near.at[side, half_at, block(k), :],
            send_sem=sent,
            recv_sem=received,
            device_id=(snap, me, other),
            device_id_type=MESH,
        )

    own = pltpu.make_async_remote_copy(
        src_ref=kept.at[core],
        dst_ref=kept.at[core],
        send_sem=send_sem.at[4, 0],
        recv_sem=sib_sem,
        device_id=(snap, me, other),
        device_id_type=MESH,
    )
    own_in = pltpu.make_async_remote_copy(
        src_ref=kept.at[other],
        dst_ref=kept.at[other],
        send_sem=send_sem.at[4, 0],
        recv_sem=sib_sem,
        device_id=(snap, me, other),
        device_id_type=MESH,
    )
    own.start()
    for k in range(CHUNKS):
        to_partner(k).start()
    own_in.wait_recv()

    def skew(first, second, m, row_base, lane_base):
        at = pl.ds(m * BLK, BLK)
        band = jnp.concatenate(
            [first[at, :], second[at, :], jnp.zeros((BLK, LANE), jnp.bfloat16)], 1
        )
        turn = (m * BLK) % LANE
        if turn:
            band = pltpu.roll(band.astype(jnp.float32), turn, 1).astype(jnp.bfloat16)
        start = lane_base + m * BLK - turn
        low = max(0, -start)
        high = min(band.shape[1], 3 * width - start)
        right[pl.ds(row_base + m * BLK, BLK), pl.ds(start + low, high - low)] = band[:, low:high]

    for m in range(block_rows):
        skew(kept.at[0], kept.at[1], m, rows, 0)

    @pl.when(jnp.logical_not(has_origin))
    def _():
        near[q_side] = jnp.zeros(near.shape[1:], near.dtype)

    for k in range(CHUNKS):
        from_partner(k).wait_recv()
        across(p_side, core, k, send_sem.at[2, k], psib_sem.at[k]).start()

        @pl.when(has_onward)
        def _():
            to_onward(k).start()

    for k in range(CHUNKS):

        @pl.when(has_origin)
        def _():
            from_origin(k).wait_recv()
            across(q_side, core, k, send_sem.at[3, k], qsib_sem.at[k]).start()

        across(p_side, other, k, send_sem.at[2, k], psib_sem.at[k]).wait_recv()

    @pl.when(has_origin)
    def _():
        for k in range(CHUNKS):
            across(q_side, other, k, send_sem.at[3, k], qsib_sem.at[k]).wait_recv()

    for m in range(block_rows):
        skew(near.at[0, 0], near.at[0, 1], m, 0, -width)
    for m in range(block_rows):
        skew(near.at[1, 0], near.at[1, 1], m, 2 * rows, width)

    step = width // 2
    for n in range(6):
        at = pl.ds(n * step, step)
        deep = pl.ds(rows if n >= 4 else 0, (3 if n in (2, 3) else 2) * rows)
        tile = jnp.dot(
            right[pl.ds(rows, rows), deep], right[deep, at], preferred_element_type=jnp.float32
        )
        for m in range(block_rows):
            squared[pl.ds(m * BLK, BLK), at] = (
                tile[m * BLK : (m + 1) * BLK] * keep_filter[m : m + 1, at]
            ).astype(jnp.bfloat16)

    lane = lax.broadcasted_iota(jnp.int32, (LANE, LANE), 1)
    diagonal = lane == lax.broadcasted_iota(jnp.int32, (LANE, LANE), 0)
    kept_sum = jnp.zeros((LANE, LANE), jnp.float32)
    squared_sum = jnp.zeros((LANE, LANE), jnp.float32)
    for b in range(rows // LANE):
        here = pl.ds(width + b * LANE, LANE)
        kept_sum += jnp.where(
            diagonal, right[pl.ds(rows + b * LANE, LANE), here].astype(jnp.float32), 0.0
        )
        squared_sum += jnp.where(
            diagonal, squared[pl.ds(b * LANE, LANE), here].astype(jnp.float32), 0.0
        )
    part[0] = jnp.sum(kept_sum.reshape(LANE // 8, 8, LANE), 0)
    part[1] = jnp.sum(squared_sum.reshape(LANE // 8, 8, LANE), 0)

    left = pl.multiple_of(core * width, LANE)
    for n in range(4):
        at = pl.ds(pl.multiple_of(left + n * step, LANE), step)
        tile = jnp.dot(squared[...], right[:, at], preferred_element_type=jnp.float32)
        for m in range(block_rows):
            rows_at = pl.ds(m * BLK, BLK)
            result[rows_at, pl.ds(n * step, step)] = (
                3.0 * squared[rows_at, at].astype(jnp.float32)
                - 2.0 * (tile[m * BLK : (m + 1) * BLK] * keep_filter[m : m + 1, at])
            )
        if n == 0:

            def share(step_to, _):
                peer = lax.rem(me + step_to, row_size)
                pltpu.make_async_remote_copy(
                    src_ref=part,
                    dst_ref=parts.at[step_to],
                    send_sem=tsend_sem.at[step_to],
                    recv_sem=trecv_sem.at[step_to],
                    device_id=(snap, peer, core),
                    device_id_type=MESH,
                ).start()
                return 0

            lax.fori_loop(1, row_size, share, 0)

    for m in range(block_rows):
        turn = (m * BLK) % LANE
        start = m * BLK - turn
        band = result[pl.ds(m * BLK, BLK), pl.ds(start, width + (LANE if turn else 0))]
        if turn:
            band = pltpu.roll(band, band.shape[1] - turn, 1)
        out[pl.ds(m * BLK, BLK), :] = band[:, :width].astype(jnp.bfloat16)

    def gather(step_to, sums):
        peer = lax.rem(me + row_size - step_to, row_size)
        pltpu.make_async_remote_copy(
            src_ref=part,
            dst_ref=parts.at[step_to],
            send_sem=tsend_sem.at[step_to],
            recv_sem=trecv_sem.at[step_to],
            device_id=(snap, peer, core),
            device_id_type=MESH,
        ).wait()
        return (sums[0] + parts[step_to, 0], sums[1] + parts[step_to, 1])

    sums = lax.fori_loop(1, row_size, gather, (part[0], part[1]))
    traces[0] = jnp.sum(sums[0]) / (total * BLK)
    traces[1] = jnp.sum(sums[1]) / (total * BLK)

    own.wait_send()
    for k in range(CHUNKS):
        to_partner(k).wait_send()
        across(p_side, core, k, send_sem.at[2, k], psib_sem.at[k]).wait_send()

        @pl.when(has_onward)
        def _():
            to_onward(k).wait_send()

        @pl.when(has_origin)
        def _():
            across(q_side, core, k, send_sem.at[3, k], qsib_sem.at[k]).wait_send()


def solution(mesh):
    row_size = mesh.shape["row"]

    def per_device(density, pattern, filter_mask):
        rows, width = density.shape
        block_rows = rows // BLK
        return pl.pallas_call(
            functools.partial(kernel, row_size),
            out_shape=(
                jax.ShapeDtypeStruct((rows, width), jnp.bfloat16),
                jax.ShapeDtypeStruct((2,), jnp.float32),
            ),
            in_specs=[pl.BlockSpec(memory_space=pltpu.VMEM)] * 3,
            out_specs=(
                pl.BlockSpec(memory_space=pltpu.VMEM),
                pl.BlockSpec(memory_space=pltpu.SMEM),
            ),
            scratch_shapes=[
                pltpu.VMEM((2, rows, width), jnp.bfloat16),
                pltpu.VMEM((2, 2, rows, width), jnp.bfloat16),
                pltpu.VMEM((3 * rows, 3 * width), jnp.bfloat16),
                pltpu.VMEM((rows, 3 * width), jnp.bfloat16),
                pltpu.VMEM((block_rows, 3 * width), jnp.float32),
                pltpu.VMEM((rows, 2 * width), jnp.float32),
                pltpu.VMEM((2, 8, LANE), jnp.float32),
                pltpu.VMEM((row_size, 2, 8, LANE), jnp.float32),
                pltpu.SemaphoreType.DMA((5, CHUNKS)),
                pltpu.SemaphoreType.DMA,
                pltpu.SemaphoreType.DMA((CHUNKS,)),
                pltpu.SemaphoreType.DMA((CHUNKS,)),
                pltpu.SemaphoreType.DMA((CHUNKS,)),
                pltpu.SemaphoreType.DMA((CHUNKS,)),
                pltpu.SemaphoreType.DMA((row_size,)),
                pltpu.SemaphoreType.DMA((row_size,)),
            ],
            compiler_params=pltpu.CompilerParams(
                collective_id=0, has_side_effects=True, vmem_limit_bytes=56 * 1024 * 1024
            ),
        )(density, pattern, filter_mask)

    return jax.shard_map(
        per_device,
        mesh=mesh,
        in_specs=(P(("snap", "row"), "col"), P(("snap", "row"), "col"), P(("snap", "row"), None)),
        out_specs=(P(("snap", "row"), "col"), P("snap")),
        check_vma=False,
    )
```

time: 520 us -> 33.9 us (0.07)
  local copies, waits for them, and re-layouts: 381 us -> 2.38 us
  blocking collectives: 34.8 us -> 0 us
  Pallas kernels: 0 us -> 30.7 us
  matrix products: 23.9 us -> 0 us
  waiting for transfers between devices: 22.9 us -> 0 us
  other arithmetic: 21.4 us -> 0 us
  between operations: 14.2 us -> 0.65 us
  loops' own time: 13.2 us -> 0 us
  starting transfers between devices: 6.27 us -> 0 us
    while x416 -> x0, local copies, waits for them, and re-layouts: 178 us -> none
    slice x121 -> x0, local copies, waits for them, and re-layouts: 101 us -> none  [the longest x120 98.7 us: shift_slots(): segment[:, :segment.shape[1] - moved * BLK]]
    dynamic_slice x152 -> x0, local copies, waits for them, and re-layouts: 58.1 us -> none  [the longest x136 45.4 us: one_group(): lax.dynamic_slice_in_dim(segment, first_slot * BLK, column_slots * BLK, 1)]
    psum x1 -> x0, blocking collectives: 34.8 us -> none  [per_device(): total_squared = lax.psum(trace_squared, ('row', 'col'))]
    pallas_call x0 -> x1, Pallas kernels: none -> 30.7 us  [per_device(): pl.pallas_call(functools.partial(kernel, row_size), out_shape=(jax.ShapeD...]
    dot_general x8 -> x0, matrix products: 23.9 us -> none  [one_group(): jnp.einsum('gak,gkn->gan', left_rows, gathered, preferred_element_type=jn...]
    ppermute x2 -> x0, waiting for transfers between devices: 21.1 us -> none  [the longest x1 21.1 us: extended_2(): before = lax.ppermute(last, axis, up)]
    another operation x12 -> x0, local copies, waits for them, and re-layouts: 17.4 us -> none  [the longest x2 9.95 us: expand_mask(): blocks = values.reshape(block_rows, BLK, slot_count, BLK)]
  transfers between devices with their start and end apart: 4 -> 0, of which waited for: 2 -> 0; matrix products, arithmetic and copies ran while one was open for 8% -> 0% of each run, Pallas kernels for 0% -> 0%
where the time goes in v1:
time: 33.9 us; the launch traced here: 33.7 us
  Pallas kernels  30.7 us (91%)
  local copies, waits for them, and re-layouts  2.38 us (7%)
  between operations  0.65 us (2%)
    pallas_call x1, Pallas kernels, per_device(): pl.pallas_call(functools.partial(kernel, row_size), out_shape=(jax.ShapeD...  30.7 us
    unnamed x4, local copies, waits for them, and re-layouts  2.38 us

profile of v1, /device:TPU:0, one launch (start us, length us, event | category | flops | bytes accessed | tf_op | source)
XLA Modules:
  0.0 33.7 jit_solution(3034886398776778013)
XLA Ops:
  0.6 30.7 %shard_map.50 = (bf16[512,512]{1,0:T(8,128)(2,1)}, f32[2]{0:T(128)}) custom-call(bf16[512,512]{1,0:T(8,128)(2,1)} %density.1, s32[16,16]{1,0:T(8,128)} %pattern.1, s32[16,32]{1,0:T(8,128)} %filter_mask.1), custom_call_target="tpu_custom_call" | custom-call | tf_op jit(solution)/shard_map/pallas_call | solution.py:323
  31.3 0.0 copy-start
  31.4 1.9 %copy.7 = bf16[512,512]{1,0:T(8,128)(2,1)} copy(bf16[512,512]{1,0:T(8,128)(2,1)} %get-tuple-element.4) | data formatting | bytes 1048576
  33.2 0.0 copy-done
  33.2 0.5 %copy.8 = f32[2]{0:T(128)} copy(f32[2]{0:T(128)S(1)} %copy-done) | data formatting | bytes 16
Async XLA Ops:
  31.3 1.9 %copy-start = (f32[2]{0:T(128)S(1)}, f32[2]{0:T(128)}, u32[]{:S(2)}) copy-start(f32[2]{0:T(128)} %get-tuple-element.5) | copy-start | bytes 28

commit v2 on v1

--- a/solution.py
+++ b/solution.py
@@ -10,6 +10,7 @@
 BLK = 32
 LANE = 128
 CHUNKS = 8
+LAG = 3
 MESH = pl.DeviceIdType.MESH
 
 
@@ -33,14 +34,18 @@
 
 def kernel(
     row_size,
+    density_in,
+    pattern_in,
+    filter_in,
+    out,
+    traces,
     density,
     pattern,
     filter_mask,
-    out,
-    traces,
     kept,
     near,
     right,
+    total_sum,
     squared,
     keep_filter,
     result,
@@ -54,8 +59,11 @@
     qsib_sem,
     tsend_sem,
     trecv_sem,
+    load_sem,
+    round_sem,
+    done_sem,
 ):
-    rows, width = density.shape
+    rows, width = density_in.shape
     half = width // BLK
     block_rows = rows // BLK
     chunk = rows // CHUNKS
@@ -75,32 +83,41 @@
 
     barrier = pltpu.get_barrier_semaphore()
 
-    def greet(step, _):
-        peer = lax.rem(me + step, row_size)
-        pl.semaphore_signal(barrier, inc=1, device_id=(snap, peer, core), device_id_type=MESH)
-        return 0
-
-    pl.semaphore_signal(barrier, inc=1, device_id=(snap, me, other), device_id_type=MESH)
-    lax.fori_loop(1, row_size, greet, 0)
-
+    def greet(row, column, semaphore):
+        pl.semaphore_signal(semaphore, inc=1, device_id=(snap, row, column), device_id_type=MESH)
+
+    greet(me, other, barrier)
+    greet(partner, core, barrier)
+
+    @pl.when(has_onward)
+    def _():
+        greet(onward, core, barrier)
+
+    @pl.when(has_origin)
+    def _():
+        greet(origin, core, barrier)
+
+    beside = has_onward.astype(jnp.int32) + has_origin.astype(jnp.int32)
+    loads = [
+        pltpu.make_async_copy(source, target, load_sem.at[i])
+        for i, (source, target) in enumerate(
+            ((density_in, density), (pattern_in, pattern), (filter_in, filter_mask))
+        )
+    ]
+    for load in loads:
+        load.start()
+    loads[1].wait()
     first_slot = core * half
     keep = lanes_padded(pattern[...]).astype(jnp.float32)
     keep = keep * valid_slots(me * block_rows, block_rows, first_slot, half, total)
     spread = jnp.dot(keep.astype(jnp.bfloat16), expander(width), preferred_element_type=jnp.float32)
+    loads[0].wait()
     for m in range(block_rows):
         at = pl.ds(m * BLK, BLK)
         kept[core, at, :] = (
             density[at, :].astype(jnp.float32) * spread[m : m + 1, :]
         ).astype(jnp.bfloat16)
-    keep = lanes_padded(filter_mask[...]).astype(jnp.float32)
-    keep = keep * valid_slots(me * block_rows, block_rows, 0, half, total)
-    keep = pltpu.roll(keep, 0, 1, stride=1, stride_axis=0)
-    keep_filter[...] = jnp.dot(
-        keep.astype(jnp.bfloat16), expander(3 * width), preferred_element_type=jnp.float32
-    )
-    right[...] = jnp.zeros_like(right)
-
-    pl.semaphore_wait(barrier, row_size)
+    pl.semaphore_wait(barrier, 2 + beside)
 
     def block(k):
         return pl.ds(k * chunk, chunk)
@@ -174,9 +191,18 @@
     own.start()
     for k in range(CHUNKS):
         to_partner(k).start()
+    loads[2].wait()
+    keep = lanes_padded(filter_mask[...]).astype(jnp.float32)
+    keep = keep * valid_slots(me * block_rows, block_rows, 0, half, total)
+    keep = pltpu.roll(keep, 0, 1, stride=1, stride_axis=0)
+    keep_filter[...] = jnp.dot(
+        keep.astype(jnp.bfloat16), expander(3 * width), preferred_element_type=jnp.float32
+    )
+    right[:, pl.ds(width, 3 * width)] = jnp.zeros((3 * rows, 3 * width), right.dtype)
+
     own_in.wait_recv()
 
-    def skew(first, second, m, row_base, lane_base):
+    def skew(first, second, m, side):
         at = pl.ds(m * BLK, BLK)
         band = jnp.concatenate(
             [first[at, :], second[at, :], jnp.zeros((BLK, LANE), jnp.bfloat16)], 1
@@ -184,56 +210,101 @@
         turn = (m * BLK) % LANE
         if turn:
             band = pltpu.roll(band.astype(jnp.float32), turn, 1).astype(jnp.bfloat16)
-        start = lane_base + m * BLK - turn
-        low = max(0, -start)
-        high = min(band.shape[1], 3 * width - start)
-        right[pl.ds(row_base + m * BLK, BLK), pl.ds(start + low, high - low)] = band[:, low:high]
+        to_row = pl.multiple_of(side * rows + m * BLK, BLK)
+        to_lane = pl.multiple_of(side * width + m * BLK - turn, LANE)
+        right[pl.ds(to_row, BLK), pl.ds(to_lane, 2 * width + LANE)] = band
 
     for m in range(block_rows):
-        skew(kept.at[0], kept.at[1], m, rows, 0)
+        skew(kept.at[0], kept.at[1], m, 1)
 
     @pl.when(jnp.logical_not(has_origin))
     def _():
         near[q_side] = jnp.zeros(near.shape[1:], near.dtype)
 
-    for k in range(CHUNKS):
-        from_partner(k).wait_recv()
-        across(p_side, core, k, send_sem.at[2, k], psib_sem.at[k]).start()
-
+    def meet(level, _):
         @pl.when(has_onward)
         def _():
-            to_onward(k).start()
-
-    for k in range(CHUNKS):
+            greet(onward, core, round_sem.at[level])
 
         @pl.when(has_origin)
         def _():
-            from_origin(k).wait_recv()
-            across(q_side, core, k, send_sem.at[3, k], qsib_sem.at[k]).start()
-
-        across(p_side, other, k, send_sem.at[2, k], psib_sem.at[k]).wait_recv()
-
-    @pl.when(has_origin)
-    def _():
-        for k in range(CHUNKS):
-            across(q_side, other, k, send_sem.at[3, k], qsib_sem.at[k]).wait_recv()
+            greet(origin, core, round_sem.at[level])
+
+        pl.semaphore_wait(round_sem.at[level], beside)
+        return 0
+
+    lax.fori_loop(1, row_size // 2, meet, 0)
+    greet(partner, core, done_sem)
+
+    step = width // 2
+
+    def own_product(n):
+        at = pl.ds(n * step, step)
+        total_sum[:, at] = jnp.dot(
+            right[pl.ds(rows, rows), pl.ds(2 * width, width)],
+            right[pl.ds(rows, rows), pl.ds(width + n * step, step)],
+            preferred_element_type=jnp.float32,
+        )
+
+    def side_product(side, part_at):
+        depth = rows // 2
+        from_row = pl.multiple_of(side * rows + part_at * depth, LANE)
+        from_lane = pl.multiple_of((1 + side) * width + part_at * depth, LANE)
+        to_lane = (side // 2) * width
+        for n in range(4):
+            at = pl.multiple_of(to_lane + n * step, LANE)
+            total_sum[:, pl.ds(at, step)] += jnp.dot(
+                right[pl.ds(rows, rows), pl.ds(from_lane, depth)],
+                right[pl.ds(from_row, depth), pl.ds(pl.multiple_of(width + at, LANE), step)],
+                preferred_element_type=jnp.float32,
+            )
+
+    def lay(side, k):
+        for m in range(k * chunk // BLK, (k + 1) * chunk // BLK):
+            skew(near.at[side, 0], near.at[side, 1], m, 2 * side)
+
+    for k in range(CHUNKS + LAG + 1):
+        if k < CHUNKS:
+            from_partner(k).wait_recv()
+            across(p_side, core, k, send_sem.at[2, k], psib_sem.at[k]).start()
+
+            @pl.when(has_onward)
+            def _():
+                to_onward(k).start()
+
+        if 0 <= k - LAG < CHUNKS:
+
+            @pl.when(has_origin)
+            def _():
+                from_origin(k - LAG).wait_recv()
+                across(q_side, core, k - LAG, send_sem.at[3, k - LAG], qsib_sem.at[k - LAG]).start()
+
+        if k < 6:
+            own_product(k)
+        late = k - 1
+        if 0 <= late < CHUNKS:
+            across(p_side, other, late, send_sem.at[2, late], psib_sem.at[late]).wait_recv()
+            lay(p_side, late)
+            if late == CHUNKS - 1:
+                side_product(2 * p_side, 1)
+        late = k - 1 - LAG
+        if 0 <= late < CHUNKS:
+
+            @pl.when(has_origin)
+            def _():
+                across(q_side, other, late, send_sem.at[3, late], qsib_sem.at[late]).wait_recv()
+
+            lay(q_side, late)
+        if k == max(6, CHUNKS // 2 + 1):
+            side_product(2 * p_side, 0)
+        if k == max(7, CHUNKS // 2 + 1 + LAG):
+            side_product(2 * q_side, 0)
+    side_product(2 * q_side, 1)
+    pl.semaphore_wait(done_sem, 1)
 
     for m in range(block_rows):
-        skew(near.at[0, 0], near.at[0, 1], m, 0, -width)
-    for m in range(block_rows):
-        skew(near.at[1, 0], near.at[1, 1], m, 2 * rows, width)
-
-    step = width // 2
-    for n in range(6):
-        at = pl.ds(n * step, step)
-        deep = pl.ds(rows if n >= 4 else 0, (3 if n in (2, 3) else 2) * rows)
-        tile = jnp.dot(
-            right[pl.ds(rows, rows), deep], right[deep, at], preferred_element_type=jnp.float32
-        )
-        for m in range(block_rows):
-            squared[pl.ds(m * BLK, BLK), at] = (
-                tile[m * BLK : (m + 1) * BLK] * keep_filter[m : m + 1, at]
-            ).astype(jnp.bfloat16)
+        at = pl.ds(m * BLK, BLK)
+        squared[at, :] = (total_sum[at, :] * keep_filter[m : m + 1, :]).astype(jnp.bfloat16)
 
     lane = lax.broadcasted_iota(jnp.int32, (LANE, LANE), 1)
     diagonal = lane == lax.broadcasted_iota(jnp.int32, (LANE, LANE), 0)
@@ -242,7 +313,7 @@
     for b in range(rows // LANE):
         here = pl.ds(width + b * LANE, LANE)
         kept_sum += jnp.where(
-            diagonal, right[pl.ds(rows + b * LANE, LANE), here].astype(jnp.float32), 0.0
+            diagonal, right[pl.ds(rows + b * LANE, LANE), pl.ds(2 * width + b * LANE, LANE)].astype(jnp.float32), 0.0
         )
         squared_sum += jnp.where(
             diagonal, squared[pl.ds(b * LANE, LANE), here].astype(jnp.float32), 0.0
@@ -250,15 +321,26 @@
     part[0] = jnp.sum(kept_sum.reshape(LANE // 8, 8, LANE), 0)
     part[1] = jnp.sum(squared_sum.reshape(LANE // 8, 8, LANE), 0)
 
-    left = pl.multiple_of(core * width, LANE)
     for n in range(4):
-        at = pl.ds(pl.multiple_of(left + n * step, LANE), step)
-        tile = jnp.dot(squared[...], right[:, at], preferred_element_type=jnp.float32)
+        if n < 2:
+            column = width + n * step
+            place = (1 - core) * width + n * step
+            deep = pl.ds(0, 3 * rows)
+        else:
+            column = 2 * core * width + (n - 2) * step
+            place = core * width + (n - 2) * step
+            deep = pl.ds(pl.multiple_of(core * rows, LANE), 2 * rows)
+        at = pl.ds(pl.multiple_of(column, LANE), step)
+        place = pl.ds(pl.multiple_of(place, LANE), step)
+        tile = jnp.dot(
+            squared[:, deep],
+            right[deep, pl.ds(pl.multiple_of(width + column, LANE), step)],
+            preferred_element_type=jnp.float32,
+        )
         for m in range(block_rows):
             rows_at = pl.ds(m * BLK, BLK)
-            result[rows_at, pl.ds(n * step, step)] = (
-                3.0 * squared[rows_at, at].astype(jnp.float32)
-                - 2.0 * (tile[m * BLK : (m + 1) * BLK] * keep_filter[m : m + 1, at])
+            result[rows_at, place] = 3.0 * squared[rows_at, at].astype(jnp.float32) - 2.0 * (
+                tile[m * BLK : (m + 1) * BLK] * keep_filter[pl.ds(m, 1), at]
             )
         if n == 0:
 
@@ -323,18 +405,22 @@
         return pl.pallas_call(
             functools.partial(kernel, row_size),
             out_shape=(
-                jax.ShapeDtypeStruct((rows, width), jnp.bfloat16),
+                pltpu.VMEM((rows, width), jnp.bfloat16),
                 jax.ShapeDtypeStruct((2,), jnp.float32),
             ),
-            in_specs=[pl.BlockSpec(memory_space=pltpu.VMEM)] * 3,
+            in_specs=[pl.BlockSpec(memory_space=pl.ANY)] * 3,
             out_specs=(
                 pl.BlockSpec(memory_space=pltpu.VMEM),
                 pl.BlockSpec(memory_space=pltpu.SMEM),
             ),
             scratch_shapes=[
+                pltpu.VMEM((rows, width), jnp.bfloat16),
+                pltpu.VMEM(pattern.shape, jnp.int32),
+                pltpu.VMEM(filter_mask.shape, jnp.int32),
                 pltpu.VMEM((2, rows, width), jnp.bfloat16),
                 pltpu.VMEM((2, 2, rows, width), jnp.bfloat16),
-                pltpu.VMEM((3 * rows, 3 * width), jnp.bfloat16),
+                pltpu.VMEM((3 * rows, 5 * width), jnp.bfloat16),
+                pltpu.VMEM((rows, 3 * width), jnp.float32),
                 pltpu.VMEM((rows, 3 * width), jnp.bfloat16),
                 pltpu.VMEM((block_rows, 3 * width), jnp.float32),
                 pltpu.VMEM((rows, 2 * width), jnp.float32),
@@ -348,6 +434,9 @@
                 pltpu.SemaphoreType.DMA((CHUNKS,)),
                 pltpu.SemaphoreType.DMA((row_size,)),
                 pltpu.SemaphoreType.DMA((row_size,)),
+                pltpu.SemaphoreType.DMA((3,)),
+                pltpu.SemaphoreType.REGULAR((max(row_size // 2, 1),)),
+                pltpu.SemaphoreType.REGULAR,
             ],
             compiler_params=pltpu.CompilerParams(
                 collective_id=0, has_side_effects=True, vmem_limit_bytes=56 * 1024 * 1024

time: 33.9 us -> 31.4 us (0.926)
  Pallas kernels: 30.7 us -> 29.3 us
  local copies, waits for them, and re-layouts: 2.38 us -> 1.31 us
    pallas_call x1, Pallas kernels: 30.7 us -> 29.3 us  [per_device(): pl.pallas_call(functools.partial(kernel, row_size), out_shape=(pltpu.VMEM...]
    unnamed x4, local copies, waits for them, and re-layouts: 2.38 us -> 1.31 us
where the time goes in v2:
time: 31.4 us; the launch traced here: 31.2 us
  Pallas kernels  29.3 us (93%)
  local copies, waits for them, and re-layouts  1.31 us (4%)
  between operations  0.65 us (2%)
    pallas_call x1, Pallas kernels, per_device(): pl.pallas_call(functools.partial(kernel, row_size), out_shape=(pltpu.VMEM...  29.3 us
    unnamed x4, local copies, waits for them, and re-layouts  1.31 us

profile of v2, /device:TPU:0, one launch (start us, length us, event | category | flops | bytes accessed | tf_op | source)
XLA Modules:
  0.0 31.2 jit_solution(10892791664631514728)
XLA Ops:
  0.6 29.3 %shard_map.50 = (bf16[512,512]{1,0:T(8,128)(2,1)S(1)}, f32[2]{0:T(128)}) custom-call(bf16[512,512]{1,0:T(8,128)(2,1)} %density_in.1, s32[16,16]{1,0:T(8,128)} %pattern_in.1, s32[16,32]{1,0:T(8,128)} %filter_in.1), custom_call_target="tpu_custom_call" | custom-call | tf_op jit(solution)/shard_map/pallas_call | solution.py:405
  29.9 0.0 copy-start
  29.9 0.8 %copy.7 = bf16[512,512]{1,0:T(8,128)(2,1)} copy(bf16[512,512]{1,0:T(8,128)(2,1)S(1)} %get-tuple-element.2) | data formatting | bytes 1048576
  30.7 0.0 copy-done
  30.7 0.5 %copy.8 = f32[2]{0:T(128)} copy(f32[2]{0:T(128)S(1)} %copy-done) | data formatting | bytes 16
Async XLA Ops:
  29.9 0.8 %copy-start = (f32[2]{0:T(128)S(1)}, f32[2]{0:T(128)}, u32[]{:S(2)}) copy-start(f32[2]{0:T(128)} %get-tuple-element.7) | copy-start | bytes 28

commit v3 on v2

--- a/solution.py
+++ b/solution.py
@@ -122,6 +122,27 @@
     def block(k):
         return pl.ds(k * chunk, chunk)
 
+    def lanes(k, short):
+        above = k * chunk // LANE * LANE
+        if short == 0:
+            return pl.ds(0, width)
+        if short == 1:
+            return pl.ds(0, width - above)
+        return pl.ds(rows - above - LANE, above + LANE)
+
+    def either(exists, act):
+        @pl.when(exists & (core == odd) & (odd == 1))
+        def _():
+            act(1)
+
+        @pl.when(exists & (core == odd) & (odd == 0))
+        def _():
+            act(2)
+
+        @pl.when(exists & (core != odd))
+        def _():
+            act(0)
+
     def to_partner(k):
         return pltpu.make_async_remote_copy(
             src_ref=kept.at[core, block(k), :],
@@ -142,20 +163,20 @@
             device_id_type=MESH,
         )
 
-    def to_onward(k):
+    def to_onward(k, short):
         return pltpu.make_async_remote_copy(
-            src_ref=near.at[p_side, core, block(k), :],
-            dst_ref=near.at[q_side, core, block(k), :],
+            src_ref=near.at[p_side, core, block(k), lanes(k, short)],
+            dst_ref=near.at[q_side, core, block(k), lanes(k, short)],
             send_sem=send_sem.at[1, k],
             recv_sem=q_sem.at[k],
             device_id=(snap, onward, core),
             device_id_type=MESH,
         )
 
-    def from_origin(k):
+    def from_origin(k, short):
         return pltpu.make_async_remote_copy(
-            src_ref=near.at[p_side, core, block(k), :],
-            dst_ref=near.at[q_side, core, block(k), :],
+            src_ref=near.at[p_side, core, block(k), lanes(k, short)],
+            dst_ref=near.at[q_side, core, block(k), lanes(k, short)],
             send_sem=send_sem.at[1, k],
             recv_sem=q_sem.at[k],
             device_id=(snap, origin, core),
@@ -221,7 +242,9 @@
     def _():
         near[q_side] = jnp.zeros(near.shape[1:], near.dtype)
 
-    def meet(level, _):
+    levels = row_size // 2
+
+    def meet(level):
         @pl.when(has_onward)
         def _():
             greet(onward, core, round_sem.at[level])
@@ -230,11 +253,13 @@
         def _():
             greet(origin, core, round_sem.at[level])
 
+    def met(level):
         pl.semaphore_wait(round_sem.at[level], beside)
+
+    def meet_again(level, _):
+        meet(level)
+        met(level)
         return 0
-
-    lax.fori_loop(1, row_size // 2, meet, 0)
-    greet(partner, core, done_sem)
 
     step = width // 2
 
@@ -268,17 +293,20 @@
             from_partner(k).wait_recv()
             across(p_side, core, k, send_sem.at[2, k], psib_sem.at[k]).start()
 
-            @pl.when(has_onward)
-            def _():
-                to_onward(k).start()
+            either(has_onward, lambda short: to_onward(k, short).start())
 
         if 0 <= k - LAG < CHUNKS:
+
+            either(has_origin, lambda short: from_origin(k - LAG, short).wait_recv())
 
             @pl.when(has_origin)
             def _():
-                from_origin(k - LAG).wait_recv()
                 across(q_side, core, k - LAG, send_sem.at[3, k - LAG], qsib_sem.at[k - LAG]).start()
 
+        if 1 <= k - 1 < levels:
+            met(k - 1)
+        if 1 <= k < levels:
+            meet(k)
         if k < 6:
             own_product(k)
         late = k - 1
@@ -299,12 +327,13 @@
             side_product(2 * p_side, 0)
         if k == max(7, CHUNKS // 2 + 1 + LAG):
             side_product(2 * q_side, 0)
+        if k == min(CHUNKS, levels):
+            if k < levels:
+                met(k)
+                lax.fori_loop(k + 1, levels, meet_again, 0)
+            greet(partner, core, done_sem)
     side_product(2 * q_side, 1)
     pl.semaphore_wait(done_sem, 1)
-
-    for m in range(block_rows):
-        at = pl.ds(m * BLK, BLK)
-        squared[at, :] = (total_sum[at, :] * keep_filter[m : m + 1, :]).astype(jnp.bfloat16)
 
     lane = lax.broadcasted_iota(jnp.int32, (LANE, LANE), 1)
     diagonal = lane == lax.broadcasted_iota(jnp.int32, (LANE, LANE), 0)
@@ -315,11 +344,31 @@
         kept_sum += jnp.where(
             diagonal, right[pl.ds(rows + b * LANE, LANE), pl.ds(2 * width + b * LANE, LANE)].astype(jnp.float32), 0.0
         )
-        squared_sum += jnp.where(
-            diagonal, squared[pl.ds(b * LANE, LANE), here].astype(jnp.float32), 0.0
-        )
+        blocks = []
+        for m in range(b * LANE // BLK, (b + 1) * LANE // BLK):
+            blocks.append(total_sum[pl.ds(m * BLK, BLK), here] * keep_filter[pl.ds(m, 1), here])
+        rounded = jnp.concatenate(blocks, 0).astype(jnp.bfloat16).astype(jnp.float32)
+        squared_sum += jnp.where(diagonal, rounded, 0.0)
     part[0] = jnp.sum(kept_sum.reshape(LANE // 8, 8, LANE), 0)
     part[1] = jnp.sum(squared_sum.reshape(LANE // 8, 8, LANE), 0)
+
+    for m in range(block_rows):
+        at = pl.ds(m * BLK, BLK)
+        squared[at, :] = (total_sum[at, :] * keep_filter[m : m + 1, :]).astype(jnp.bfloat16)
+
+    def share(step_to, _):
+        peer = lax.rem(me + step_to, row_size)
+        pltpu.make_async_remote_copy(
+            src_ref=part,
+            dst_ref=parts.at[step_to],
+            send_sem=tsend_sem.at[step_to],
+            recv_sem=trecv_sem.at[step_to],
+            device_id=(snap, peer, core),
+            device_id_type=MESH,
+        ).start()
+        return 0
+
+    lax.fori_loop(1, row_size, share, 0)
 
     for n in range(4):
         if n < 2:
@@ -342,21 +391,6 @@
             result[rows_at, place] = 3.0 * squared[rows_at, at].astype(jnp.float32) - 2.0 * (
                 tile[m * BLK : (m + 1) * BLK] * keep_filter[pl.ds(m, 1), at]
             )
-        if n == 0:
-
-            def share(step_to, _):
-                peer = lax.rem(me + step_to, row_size)
-                pltpu.make_async_remote_copy(
-                    src_ref=part,
-                    dst_ref=parts.at[step_to],
-                    send_sem=tsend_sem.at[step_to],
-                    recv_sem=trecv_sem.at[step_to],
-                    device_id=(snap, peer, core),
-                    device_id_type=MESH,
-                ).start()
-                return 0
-
-            lax.fori_loop(1, row_size, share, 0)
 
     for m in range(block_rows):
         turn = (m * BLK) % LANE
@@ -387,9 +421,7 @@
         to_partner(k).wait_send()
         across(p_side, core, k, send_sem.at[2, k], psib_sem.at[k]).wait_send()
 
-        @pl.when(has_onward)
-        def _():
-            to_onward(k).wait_send()
+        either(has_onward, lambda short: to_onward(k, short).wait_send())
 
         @pl.when(has_origin)
         def _():

time: 31.4 us -> 30 us (0.955)
  Pallas kernels: 29.3 us -> 27.9 us
    pallas_call x1, Pallas kernels: 29.3 us -> 27.9 us  [per_device(): pl.pallas_call(functools.partial(kernel, row_size), out_shape=(pltpu.VMEM...]
where the time goes in v3:
time: 30 us; the launch traced here: 29.8 us
  Pallas kernels  27.9 us (93%)
  local copies, waits for them, and re-layouts  1.31 us (4%)
  between operations  0.65 us (2%)
    pallas_call x1, Pallas kernels, per_device(): pl.pallas_call(functools.partial(kernel, row_size), out_shape=(pltpu.VMEM...  27.9 us
    unnamed x4, local copies, waits for them, and re-layouts  1.31 us

profile of v3, /device:TPU:0, one launch (start us, length us, event | category | flops | bytes accessed | tf_op | source)
XLA Modules:
  0.0 29.8 jit_solution(559757458673138678)
XLA Ops:
  0.6 27.9 %shard_map.50 = (bf16[512,512]{1,0:T(8,128)(2,1)S(1)}, f32[2]{0:T(128)}) custom-call(bf16[512,512]{1,0:T(8,128)(2,1)} %density_in.1, s32[16,16]{1,0:T(8,128)} %pattern_in.1, s32[16,32]{1,0:T(8,128)} %filter_in.1), custom_call_target="tpu_custom_call" | custom-call | tf_op jit(solution)/shard_map/pallas_call | solution.py:437
  28.5 0.0 copy-start
  28.5 0.8 %copy.7 = bf16[512,512]{1,0:T(8,128)(2,1)} copy(bf16[512,512]{1,0:T(8,128)(2,1)S(1)} %get-tuple-element.2) | data formatting | bytes 1048576
  29.3 0.0 copy-done
  29.3 0.5 %copy.8 = f32[2]{0:T(128)} copy(f32[2]{0:T(128)S(1)} %copy-done) | data formatting | bytes 16
Async XLA Ops:
  28.5 0.8 %copy-start = (f32[2]{0:T(128)S(1)}, f32[2]{0:T(128)}, u32[]{:S(2)}) copy-start(f32[2]{0:T(128)} %get-tuple-element.7) | copy-start | bytes 28
